TPU v7x, 512 devices: a whole 4x8x8 slice. The times are simulated.
512 devices in a mesh: gx: 32 (over z_hi, x, core), gy: 16 (over y, z_lo).
Axes of the slice: x: 4, y: 8, z: 8 (z_hi: 4, z_lo: 2; z = z_hi * 2 + z_lo), core: 2. Of those that a mesh axis runs over, the one named last changes fastest.
Arguments:
- populations: float32 [19, 256, 256, 128], P(None, 'gx', 'gy')
- anchor: int32 [32, 16, 1024], P('gx', 'gy'), may hold values from 0 to 20606, as said below
- offsets: float32 [32, 16, 3, 1024], P('gx', 'gy'), may hold values from 0 to 0.999
- heading: float32 [32, 16, 2, 1024], P('gx', 'gy'), may hold values from -3.140625 to 3.140625
- velocity: float32 [32, 16, 3, 1024], P('gx', 'gy'), may hold values from -0.6 to 0.6
- live_count: int32 [32, 16], P('gx', 'gy'), may hold values from 1 to 1024, as said below
Outputs:
- populations_next: float32 [19, 256, 256, 128], P(None, 'gx', 'gy')
- swimmer_force: float32 [32, 16, 3, 1024], P('gx', 'gy')
Inputs may be any that keep to these rules, and one draw needn't show every extreme that they name: The anchor is (ax (18) + ay) * 128 + az with 0 <= ax <= 8, 0 <= ay <= 16, 0 <= az <= 126. Live swimmers fill slots 0 to live_count - 1 of their device; some device holds 1024.
All inputs are finite; a program needn't handle non-finite values.
Results may differ from a plain program's by a relative error of at most 0.0003.
Values sent between devices are 32-bit elements; how exact they have to be, the bound alone decides.
A program may use at most 64 MiB of HBM per device.

v0:
```python
import functools

import jax
import jax.numpy as jnp
import numpy as np
from jax import lax
from jax.experimental import pallas as pl
from jax.experimental.pallas import tpu as pltpu
from jax.sharding import PartitionSpec as P

DIRS = (
    (0, 0, 0), (1, 0, 0), (-1, 0, 0), (0, 1, 0), (0, -1, 0), (0, 0, 1), (0, 0, -1),
    (1, 1, 0), (-1, -1, 0), (1, -1, 0), (-1, 1, 0), (1, 0, 1), (-1, 0, -1),
    (1, 0, -1), (-1, 0, 1), (0, 1, 1), (0, -1, -1), (0, 1, -1), (0, -1, 1),
)
WEIGHTS = (1.0 / 3.0,) + (1.0 / 18.0,) * 6 + (1.0 / 36.0,) * 12
CUTOFF = 2.0 ** (1.0 / 3.0)
REACH = 1.125
FAR = 1.0e9
F32 = jnp.float32
BF16 = jnp.bfloat16
MESH = pl.DeviceIdType.MESH

CX, CY, NZ, SW = 8, 16, 128, 1024
ROWS = CX * CY
LANE_TILES = SW // 128

SIDES = ((-1, 0), (1, 0), (0, -1), (0, 1), (-1, -1), (-1, 1), (1, -1), (1, 1))
RANGES = ((0, 4, 7), (1, 0, 3), (2, 2, 5), (3, 6, 8), (3, 0, 1), (4, 4, 5), (5, 6, 7), (6, 2, 3), (7, 0, 1))


def facing(axis, sign):
    return [q for q in range(19) if DIRS[q][axis] == sign]


def corner_q(sx, sy):
    return DIRS.index((-sx, -sy, 0))


def split2(v):
    hi = v.astype(BF16)
    return hi, (v - hi.astype(F32)).astype(BF16)


def split3(v):
    hi = v.astype(BF16)
    rest = v - hi.astype(F32)
    mid = rest.astype(BF16)
    return hi, mid, (rest - mid.astype(F32)).astype(BF16)


def dot(a, b):
    return lax.dot_general(a, b, (((1,), (0,)), ((), ())), preferred_element_type=F32)


def dot_t(a, b):
    return lax.dot_general(a, b, (((1,), (1,)), ((), ())), preferred_element_type=F32)


def tent(d):
    return jnp.maximum(1.0 - jnp.abs(d), 0.0)


def moments(load):
    rho = None
    mom = [None, None, None]
    for q in range(19):
        f = load(q)
        rho = f if rho is None else rho + f
        for c in range(3):
            s = DIRS[q][c]
            if s:
                if mom[c] is None:
                    mom[c] = f if s > 0 else -f
                else:
                    mom[c] = mom[c] + f if s > 0 else mom[c] - f
    return rho, mom


def pair_terms(ox, oy, oz, px, py, pz):
    dx = ox - px
    dy = oy - py
    dz = oz - pz
    dz = dz - NZ * jnp.round(dz * (1.0 / NZ))
    raw = dx * dx + dy * dy + dz * dz
    inv = 1.0 / jnp.maximum(raw, 0.8)
    sixth = inv * inv * inv
    mag = (sixth + sixth - 1.0) * (sixth * inv)
    mag = jnp.where(raw < CUTOFF, mag, 0.0)
    return mag * dx, mag * dy, mag * dz


def classes(x, y, live):
    xl, xh = x < REACH, x > CX - 1 - REACH
    yl, yh = y < REACH, y > CY - 1 - REACH
    yc = jnp.where(yl, 0.0, jnp.where(yh, 2.0, 1.0))
    kind = jnp.where(xl, yc, jnp.where(xh, 6.0 - yc, jnp.where(yl, 7.0, jnp.where(yh, 3.0, 8.0))))
    return jnp.where(live > 0.0, kind, 9.0)


def sort_ranks(kind):
    masks = [(kind == k).astype(F32) for k in range(10)]
    ri = lax.broadcasted_iota(jnp.int32, (128, 256), 0)
    ci = lax.broadcasted_iota(jnp.int32, (128, 256), 1)
    upper = ((ri < ci) | (ci >= 128)).astype(F32).astype(BF16)
    pre = dot(jnp.concatenate(masks, axis=0).astype(BF16), upper)
    within, tile_sum = pre[:, :128], pre[:, 128:]
    place = lax.broadcasted_iota(jnp.int32, (80, 128), 0) & 7
    upto = tile_sum
    for by in (1, 2, 4):
        upto = upto + jnp.where(place >= by, pltpu.roll(upto, by, 0), 0.0)
    lane = lax.broadcasted_iota(jnp.int32, (1, 128), 1)
    rank = jnp.zeros((8, 128), F32)
    row = jnp.zeros((1, 128), F32)
    first = jnp.zeros((1, 128), F32)
    for k in range(10):
        cut = slice(8 * k, 8 * k + 8)
        row = jnp.where(lane == k, first, row)
        rank = rank + masks[k] * (within[cut] + (upto[cut] - tile_sum[cut]) + first)
        first = first + upto[8 * k + 7:8 * k + 8]
    return rank, row


def plane_weights(px, py, far):
    x8 = lax.broadcasted_iota(jnp.int32, (CX, 1), 0).astype(F32)
    y16 = lax.broadcasted_iota(jnp.int32, (CY, 1), 0).astype(F32)
    ki = lax.broadcasted_iota(jnp.int32, (16, 1), 0)
    ii, jj = lax.shift_right_logical(ki, 2), ki & 3
    xd = jnp.where(ii < 2, ii - 2, ii + CX - 2).astype(F32)
    yd = jnp.where(jj < 2, jj - 2, jj + CY - 2).astype(F32)
    tx, ty = tent(x8 - px), tent(y16 - py)
    parts = [tx[i:i + 1] * ty for i in range(CX)]
    parts += [tent(-1.0 - px) * ty, tent(CX - px) * ty, tent(-1.0 - py) * tx, tent(CY - py) * tx]
    parts += [tent(xd - px) * tent(yd - py)]
    if far:
        parts += [tent(-2.0 - px) * ty, tent(CX + 1.0 - px) * ty, tent(-2.0 - py) * tx, tent(CY + 1.0 - py) * tx]
    return jnp.concatenate(parts, axis=0)


def z_weights(pz):
    zi = lax.broadcasted_iota(jnp.int32, (NZ, 1), 0).astype(F32)
    return split2(tent(zi - pz))


def widen(v):
    hi, lo = split2(v)
    return jnp.concatenate([hi, lo], axis=1)


def sample(u, zh, zl):
    return dot(u, jnp.concatenate([zh, zh], axis=0)) + dot(u[:, :128], zl)


def columns(cols, at, place):
    turned = jnp.transpose(place)
    for c in range(3):
        cols[c, at:at + 128] = jnp.broadcast_to(turned[:, c:c + 1], (128, 128))


def pair_step(cols, mine, width):
    def step(n, acc):
        at = pl.multiple_of(n * 8, 8)
        p = [jnp.concatenate([cols[c, pl.ds(at, 8)]] * (width // 128), axis=1) for c in range(3)]
        return tuple(a + b for a, b in zip(acc, pair_terms(*mine, *p)))

    return step


def exchange_kernel(n_gx, n_gy, pops_hbm, anchor_hbm, offsets_hbm, heading_hbm, velocity_hbm, count_hbm,
                    pops, halo_x, halo_y, halo_c, lists, starts_out, own_out, base_out, mom, inner, zhl, plane,
                    anchor, offsets, heading, velocity, count, table,
                    msg_x, msg_y, msg_c, msg_l, msg_s, cols, load_sem, send_sem, recv_sem):
    gx = lax.axis_index("gx")
    gy = lax.axis_index("gy")

    def device(side):
        return (lax.rem(gx + side[0] + n_gx, n_gx), lax.rem(gy + side[1] + n_gy, n_gy))

    loads = [pltpu.make_async_copy(a, b, load_sem.at[k]) for k, (a, b) in enumerate((
        (anchor_hbm, anchor), (offsets_hbm, offsets), (heading_hbm, heading), (velocity_hbm, velocity),
        (count_hbm, count)))]
    loads += [pltpu.make_async_copy(pops_hbm.at[pl.ds(q, n)], pops.at[pl.ds(q, n)], load_sem.at[5 + k])
              for k, (q, n) in enumerate(((0, 5), (5, 5), (10, 5), (15, 4)))]
    for c in loads:
        c.start()
    barrier = pltpu.get_barrier_semaphore()
    for side in SIDES:
        pl.semaphore_signal(barrier, inc=1, device_id=device(side), device_id_type=MESH)
    for c in loads:
        c.wait()

    root = anchor[...]
    bxf = lax.shift_right_logical(root, 7).astype(F32)
    cxf = jnp.floor(bxf * (1.0 / (CY + 2)) + 0.01)
    x = cxf - 1.0 + offsets[0:8]
    y = bxf - cxf * (CY + 2) - 1.0 + offsets[8:16]
    z = (root & (NZ - 1)).astype(F32) + offsets[16:24]
    lane = lax.broadcasted_iota(jnp.int32, (8, 128), 1)
    sub = lax.broadcasted_iota(jnp.int32, (8, 128), 0)
    live = (sub * 128 + lane < count[0]).astype(F32)
    first, second = heading[pl.ds(0, 8, stride=2)], heading[pl.ds(1, 8, stride=2)]
    c1 = jnp.cos(second)
    w = [2.0 * velocity[0:8] - 0.5 * (jnp.cos(first) * c1),
         2.0 * velocity[8:16] - 0.5 * (jnp.sin(first) * c1),
         2.0 * velocity[16:24] - 0.5 * jnp.sin(second)]
    for k, v in enumerate((x, y, z, *w, live, jnp.zeros((8, 128), F32))):
        table[pl.ds(k, 8, stride=8)] = v
    rank, row = sort_ranks(classes(x, y, live))
    msg_s[...] = row
    starts_out[8] = row
    to_tile = jnp.floor(rank * (1.0 / 128.0))
    to_lane = rank - 128.0 * to_tile
    split = [v.astype(F32) for v in split3(table[...])]
    dst = lax.broadcasted_iota(jnp.int32, (128, 128), 0).astype(F32)
    ordered = jnp.zeros((24 * LANE_TILES, 128), F32)
    for t in range(0, LANE_TILES, 2):
        hot, rows = [], []
        for j in (t, t + 1):
            hot.append((dst == to_lane[j:j + 1]).astype(F32).astype(BF16))
            part = jnp.concatenate([v[8 * j:8 * j + 8] for v in split], axis=0)
            rows.append(jnp.concatenate(
                [jnp.where(to_tile[j:j + 1] == float(k), part, 0.0) for k in range(LANE_TILES)],
                axis=0).astype(BF16))
        ordered = ordered + dot_t(jnp.concatenate(rows, axis=1), jnp.concatenate(hot, axis=1))
    for t in range(LANE_TILES):
        at = 24 * t
        msg_l[t] = ordered[at:at + 8] + ordered[at + 8:at + 16] + ordered[at + 16:at + 24]

    rho, m = moments(lambda q: pops[q])
    inv = 1.0 / rho
    mom[0] = rho
    for c in range(3):
        mom[1 + c] = m[c] * inv
    for s, (adj, far) in enumerate(((0, 1), (CX - 1, CX - 2))):
        for c in range(4):
            msg_x[s, c] = mom[c, adj * CY:(adj + 1) * CY]
        for c in range(3):
            msg_x[s, 4 + c] = mom[1 + c, far * CY:(far + 1) * CY]
        for k, q in enumerate(facing(0, 2 * s - 1)):
            msg_x[s, 7 + k] = pops[q, adj * CY:(adj + 1) * CY]
    for s, (adj, far) in enumerate(((0, 1), (CY - 1, CY - 2))):
        for c in range(4):
            msg_y[s, c] = mom[c, pl.ds(adj, CX, stride=CY)]
        for c in range(3):
            msg_y[s, 4 + c] = mom[1 + c, pl.ds(far, CX, stride=CY)]
        for k, q in enumerate(facing(1, 2 * s - 1)):
            msg_y[s, 7 + k] = pops[q, pl.ds(adj, CX, stride=CY)]
    for i in range(4):
        sx, sy = SIDES[4 + i]
        ax, fx = (0, 1) if sx < 0 else (CX - 1, CX - 2)
        ay, fy = (0, 1) if sy < 0 else (CY - 1, CY - 2)
        msg_c[i] = jnp.zeros((16, 128), F32)
        for c in range(4):
            msg_c[i, c:c + 1] = mom[c, ax * CY + ay:ax * CY + ay + 1]
        for j, (nx, ny) in enumerate(((ax, fy), (fx, ay), (fx, fy))):
            for c in range(3):
                msg_c[i, 5 + 3 * j + c:6 + 3 * j + c] = mom[1 + c, nx * CY + ny:nx * CY + ny + 1]
        q = DIRS.index((sx, sy, 0))
        msg_c[i, 4:5] = pops[q, ax * CY + ay:ax * CY + ay + 1]

    def send(k, a, b, side, o):
        d = SIDES.index(side)
        return pltpu.make_async_remote_copy(
            src_ref=a, dst_ref=b, send_sem=send_sem.at[3 * d + k], recv_sem=recv_sem.at[3 * o + k],
            device_id=device(side), device_id_type=MESH)

    fluid, swimmers = [], []
    for d, side in enumerate(SIDES):
        o = SIDES.index((-side[0], -side[1]))
        if side[1] == 0:
            fluid.append(send(0, msg_x.at[d], halo_x.at[o], side, o))
        elif side[0] == 0:
            fluid.append(send(0, msg_y.at[d - 2], halo_y.at[o - 2], side, o))
        else:
            fluid.append(send(0, msg_c.at[d - 4], halo_c.at[o - 4], side, o))
        swimmers.append(send(1, msg_s, starts_out.at[o], side, o))
        swimmers.append(send(2, msg_l.at[:, pl.ds(0, 6)], lists.at[o, :, pl.ds(0, 6)], side, o))
    pl.semaphore_wait(barrier, 8)
    for c in fluid + swimmers:
        c.start()

    for c in range(3):
        inner[c * ROWS:(c + 1) * ROWS] = widen(mom[1 + c])
    for i in range(BLOCKS):
        n = BLOCK // 128
        vals = jnp.concatenate([table[8 * (n * i + j):8 * (n * i + j) + 8] for j in range(n)], axis=1)
        zh, zl = z_weights(vals[2:3])
        zhl[i, 0:NZ] = zh
        zhl[i, NZ:2 * NZ] = zl
        plane[i] = plane_weights(vals[0:1], vals[1:2], False)
        got = sample(inner[...], zh, zl)
        rows = [vals[0:3]]
        for c in range(3):
            s = jnp.sum(got[c * ROWS:(c + 1) * ROWS] * plane[i, 0:ROWS], axis=0, keepdims=True)
            rows.append((vals[3 + c:4 + c] - 2.0 * s) * vals[6:7])
        rows = jnp.concatenate(rows + [vals[6:8]], axis=0)
        for j in range(BLOCK // OWN):
            own_out[i * (BLOCK // OWN) + j] = rows[:, j * OWN:(j + 1) * OWN]

    for t in range(LANE_TILES):
        v = table[8 * t:8 * t + 8]
        columns(cols, t * 128, jnp.where((sub == 0) & (v[6:7] == 0.0), FAR, v))
    for i in range(0, SW // OWN, 2):
        width = 2 * OWN
        mine = [jnp.broadcast_to(jnp.concatenate([own_out[i, c:c + 1], own_out[i + 1, c:c + 1]], axis=1), (8, width))
                for c in range(3)]
        init = tuple(jnp.zeros((8, width), F32) for _ in range(3))
        got = lax.fori_loop(0, SW // 8, pair_step(cols, mine, width), init)
        for c in range(3):
            pairs = 0.24 * jnp.sum(got[c], axis=0, keepdims=True)
            for j in range(2):
                base_out[i + j, c:c + 1] = (pairs[:, j * OWN:(j + 1) * OWN] * own_out[i + j, 6:7]
                                            - own_out[i + j, 3 + c:4 + c])
    for i in range(SW // OWN):
        base_out[i, 3:8] = jnp.zeros((5, OWN), F32)

    for c in fluid + swimmers:
        c.wait()


ADJ = 64
FAR_ROWS = 48
ADJ_ROWS = ROWS + ADJ
BLOCK = 512
BLOCKS = SW // BLOCK
OWN = 256
GHOST_TILES = 8 * LANE_TILES + 4


def fluid_kernel(pops, own, base, halo_x, halo_y, halo_c, lists, starts_in, mom, inner, zhl, plane,
                 next_out, force_out,
                 acc, out_v, force_v, starts, node, near, outer, force, ghosts, cols, out_sem, start_sem, force_sem):
    start_copy = pltpu.make_async_copy(starts_in, starts, start_sem)
    start_copy.start()
    acc[...] = base[...]
    ghosts[...] = jnp.zeros(ghosts.shape, F32)
    force[...] = jnp.zeros(force.shape, F32)
    for c in range(3):
        corner = []
        for i in range(4):
            for j in range(4):
                sx, sy = (0 if i < 2 else 1), (0 if j < 2 else 1)
                fx, fy = i in (0, 3), j in (0, 3)
                k = 2 * sx + sy
                r = (11 if fy else 8) if fx else (5 if fy else 1)
                corner.append(halo_c[k, r + c:r + c + 1])
        near[c * ADJ:(c + 1) * ADJ] = widen(jnp.concatenate(
            [halo_x[0, 1 + c], halo_x[1, 1 + c], halo_y[0, 1 + c], halo_y[1, 1 + c]] + corner, axis=0))
        outer[c * FAR_ROWS:(c + 1) * FAR_ROWS] = widen(jnp.concatenate(
            [halo_x[0, 4 + c], halo_x[1, 4 + c], halo_y[0, 4 + c], halo_y[1, 4 + c]], axis=0))

    def spread(weights, react, zz):
        zh = zz[0:NZ]
        for c in range(3):
            wh, wl = split2(weights * react[c])
            both = dot_t(wh, zz)
            force[c] = force[c] + (both[:, :128] + both[:, 128:] + dot_t(wl, zh))

    per = BLOCK // OWN

    def own_block(i, carry):
        zz = zhl[i]
        got = sample(near[...], zz[0:NZ], zz[NZ:2 * NZ])
        vals = jnp.concatenate([own[per * i + j] for j in range(per)], axis=1)
        react = []
        for c in range(3):
            s = jnp.sum(got[c * ADJ:(c + 1) * ADJ] * plane[i, ROWS:ADJ_ROWS], axis=0, keepdims=True)
            s = 2.0 * s * vals[6:7]
            react.append(vals[3 + c:4 + c] - s)
            for j in range(per):
                acc[per * i + j, c:c + 1] = acc[per * i + j, c:c + 1] + s[:, j * OWN:(j + 1) * OWN]
        spread(plane[i], react, zz)
        return carry

    own_block(0, 0)
    start_copy.wait()
    n_own = starts[8, 0, 9].astype(jnp.int32)

    lane = lax.broadcasted_iota(jnp.int32, (8, 128), 1)
    sub = lax.broadcasted_iota(jnp.int32, (8, 128), 0)
    total = jnp.int32(0)
    puts, rest = [], []
    for d, lo, hi in RANGES:
        a = starts[d, 0, lo].astype(jnp.int32)
        b = starts[d, 0, hi].astype(jnp.int32)
        sx, sy = SIDES[d]
        moved = jnp.where(sub == 0, float(sx * CX), jnp.where(sub == 1, float(sy * CY), 0.0))
        by = (total - a) & 127
        upper = lane >= by

        def taken(t, d=d, a=a, b=b, by=by, moved=moved):
            at = t * 128 + lane
            v = jnp.where((at >= a) & (at < b), lists[d, jnp.minimum(t, LANE_TILES - 1)] + moved, 0.0)
            return pltpu.roll(v, by, 1)

        t0 = lax.shift_right_logical(a, 7)
        tile = lax.shift_right_logical(total - a + t0 * 128 + 1024, 7) - 8
        v0, v1 = taken(t0), taken(t0 + 1)
        puts.append((jnp.maximum(tile, 0), jnp.where(upper, v0, 0.0)))
        puts.append((tile + 1, jnp.where(upper, v1, v0)))
        puts.append((tile + 2, jnp.where(upper, 0.0, v1)))

        def more(t, carry, taken=taken, upper=upper, shift=tile - t0):
            v = taken(t)
            ghosts[t + shift] = ghosts[t + shift] + jnp.where(upper, v, 0.0)
            ghosts[t + shift + 1] = ghosts[t + shift + 1] + jnp.where(upper, 0.0, v)
            return carry

        rest.append((t0 + 2, lax.shift_right_logical(b + 127, 7), more))
        total = total + (b - a)
    for at, v in puts:
        ghosts[at] = ghosts[at] + v
    for lo, hi, more in rest:
        lax.fori_loop(lo, hi, more, 0)

    slot = lax.broadcasted_iota(jnp.int32, (1, BLOCK), 1)
    tiles = lax.shift_right_logical(total + 127, 7)
    ahead = BLOCK // 128

    def ghost_columns(t, carry):
        g = jnp.where((sub == 0) & (lane + t * 128 >= total), FAR, ghosts[t])
        turned = jnp.transpose(g)
        at = t * 128 if isinstance(t, int) else pl.multiple_of(t * 128, 128)
        for c in range(3):
            cols[c, pl.ds(at, 128)] = jnp.broadcast_to(turned[:, c:c + 1], (128, 128))
        return carry

    def ghost_block(i, carry):
        vals = jnp.concatenate([ghosts[ahead * i + j] for j in range(ahead)], axis=1)
        live = (slot + i * BLOCK < total).astype(F32)
        zh, zl = z_weights(vals[2:3])
        weights = plane_weights(vals[0:1], vals[1:2], True)
        gi = sample(inner[...], zh, zl)
        gn = sample(near[...], zh, zl)
        gf = sample(outer[...], zh, zl)
        react = []
        for c in range(3):
            s = (jnp.sum(gi[c * ROWS:(c + 1) * ROWS] * weights[0:ROWS], axis=0, keepdims=True)
                 + jnp.sum(gn[c * ADJ:(c + 1) * ADJ] * weights[ROWS:ADJ_ROWS], axis=0, keepdims=True)
                 + jnp.sum(gf[c * FAR_ROWS:(c + 1) * FAR_ROWS] * weights[ADJ_ROWS:], axis=0, keepdims=True))
            react.append((vals[3 + c:4 + c] - 2.0 * s) * live)
        spread(weights[0:ADJ_ROWS], react, jnp.concatenate([zh, zl], axis=0))
        return carry

    for t in range(ahead):
        ghost_columns(t, 0)
    ghost_block(0, 0)
    lax.fori_loop(ahead, tiles, ghost_columns, 0)
    lax.fori_loop(1, lax.shift_right_logical(total + BLOCK - 1, 9), ghost_block, 0)
    lax.fori_loop(1, lax.shift_right_logical(n_own + BLOCK - 1, 9), own_block, 0)

    def ghost_pairs(i, carry):
        mine = [jnp.broadcast_to(own[i, c:c + 1], (8, OWN)) for c in range(3)]
        one = pair_step(cols, mine, OWN)
        init = tuple(jnp.zeros((8, OWN), F32) for _ in range(3))

        def four(n, got):
            for k in range(4):
                got = one(4 * n + k, got)
            return got

        got = lax.fori_loop(0, lax.shift_right_logical(total + 31, 5), four, init)
        live = own[i, 6:7]
        for c in range(3):
            acc[i, c:c + 1] = acc[i, c:c + 1] + 0.24 * live * jnp.sum(got[c], axis=0, keepdims=True)
        return carry

    lax.fori_loop(0, lax.shift_right_logical(n_own + OWN - 1, 8), ghost_pairs, 0)
    for i in range(SW // OWN):
        for c in range(3):
            for j in range(2):
                r = c * LANE_TILES + 2 * i + j
                force_v[r:r + 1] = acc[i, c:c + 1, j * 128:(j + 1) * 128]
    force_copy = pltpu.make_async_copy(force_v, force_out, force_sem)
    force_copy.start()

    def prepare(rho, u0, half, g):
        u = [u0[c] + half * g[c] for c in range(3)]
        uu = u[0] * u[0] + u[1] * u[1] + u[2] * u[2]
        ug = u[0] * g[0] + u[1] * g[1] + u[2] * g[2]
        k0 = 1.25 * rho * (1.0 - 1.5 * uu) - 1.125 * ug
        return k0, 3.75 * rho, 5.625 * rho, u, [1.125 * v for v in g]

    def along(q, v):
        out = None
        for c in range(3):
            s = DIRS[q][c]
            if s:
                out = (v[c] if s > 0 else -v[c]) if out is None else (out + v[c] if s > 0 else out - v[c])
        return out

    def post(q, f, prep):
        k0, r1, r2, u, g = prep
        if q == 0:
            return -0.25 * f + WEIGHTS[0] * k0
        a, p = along(q, u), along(q, g)
        return -0.25 * f + WEIGHTS[q] * (k0 + a * (r1 + r2 * a + 3.0 * p) + p)

    def side_prep(rho, u0, lo, n):
        g = [force[c, lo:lo + n] for c in range(3)]
        return prepare(rho, u0, 0.5 / rho, g)

    k0, r1, r2, u, g = side_prep(mom[0], [mom[1 + c] for c in range(3)], 0, ROWS)
    node[0] = k0
    for c in range(3):
        node[1 + c] = u[c]
        node[4 + c] = g[c]
    xs = [side_prep(halo_x[s, 0], [halo_x[s, 1 + c] for c in range(3)], ROWS + s * CY, CY) for s in range(2)]
    ys = [side_prep(halo_y[s, 0], [halo_y[s, 1 + c] for c in range(3)], ROWS + 2 * CY + s * CX, CX)
          for s in range(2)]
    cs = []
    for i in range(4):
        sx, sy = SIDES[4 + i]
        r = ADJ_ROWS - 16 + (1 if sx < 0 else 2) * 4 + (1 if sy < 0 else 2)
        cs.append(side_prep(halo_c[i, 0:1], [halo_c[i, 1 + c:2 + c] for c in range(3)], r, 1))
    stores = []
    for q in range(19):
        dx, dy, dz = DIRS[q]
        rho_q = mom[0]
        prep = (node[0], 3.75 * rho_q, 5.625 * rho_q, [node[1 + c] for c in range(3)], [node[4 + c] for c in range(3)])

        def turned(v, dz=dz):
            return pltpu.roll(v, dz % NZ, 1) if dz else v

        v = turned(post(q, pops[q], prep))
        if dy:
            v = pltpu.roll(v, dy % ROWS, 0)
        if dx == 0:
            out_v[q] = v
        else:
            s = 0 if dx > 0 else 1
            e = turned(post(q, halo_x[s, 7 + facing(0, dx).index(q)], xs[s]))
            if dy:
                e = pltpu.roll(e, dy % CY, 0)
            if dx > 0:
                out_v[q, CY:ROWS] = v[0:ROWS - CY]
                out_v[q, 0:CY] = e
            else:
                out_v[q, 0:ROWS - CY] = v[CY:ROWS]
                out_v[q, ROWS - CY:ROWS] = e
        if dy:
            s = 0 if dy > 0 else 1
            at = 0 if dy > 0 else CY - 1
            e = turned(post(q, halo_y[s, 7 + facing(1, dy).index(q)], ys[s]))
            if dx:
                e = pltpu.roll(e, dx % CX, 0)
            out_v[q, pl.ds(at, CX, stride=CY)] = e
            if dx:
                i = SIDES.index((-dx, -dy)) - 4
                r = at + (0 if dx > 0 else (CX - 1) * CY)
                out_v[q, r:r + 1] = post(q, halo_c[i, 4:5], cs[i])
        c = pltpu.make_async_copy(out_v.at[q], next_out.at[q], out_sem.at[q])
        c.start()
        stores.append(c)
    force_copy.wait()
    for c in stores:
        c.wait()


def body(n_gx, n_gy, populations, anchor, offsets, heading, velocity, live_count):
    pops = populations.reshape(19, ROWS, NZ)
    tiles = LANE_TILES
    vmem = pl.BlockSpec(memory_space=pltpu.VMEM)
    hbm = pl.BlockSpec(memory_space=pltpu.HBM)
    dma = pltpu.SemaphoreType.DMA
    held = (
        pltpu.VMEM((19, ROWS, NZ), F32),
        pltpu.VMEM((2, 12, CY, 128), F32),
        pltpu.VMEM((2, 12, CX, 128), F32),
        pltpu.VMEM((4, 16, 128), F32),
        pltpu.VMEM((8, LANE_TILES, 8, 128), F32),
        pltpu.VMEM((9, 1, 128), F32),
        pltpu.VMEM((SW // OWN, 8, OWN), F32),
        pltpu.VMEM((SW // OWN, 8, OWN), F32),
        pltpu.VMEM((4, ROWS, NZ), F32),
        pltpu.VMEM((3 * ROWS, 2 * NZ), BF16),
        pltpu.VMEM((BLOCKS, 2 * NZ, BLOCK), BF16),
        pltpu.VMEM((BLOCKS, ADJ_ROWS, BLOCK), F32),
    )
    pops, halo_x, halo_y, halo_c, lists, starts, own, base, mom, inner, zhl, plane = pl.pallas_call(
        functools.partial(exchange_kernel, n_gx, n_gy),
        out_shape=held,
        in_specs=[hbm] * 6,
        out_specs=[vmem] * 12,
        scratch_shapes=[
            pltpu.VMEM((tiles, 128), jnp.int32),
            pltpu.VMEM((3 * tiles, 128), F32),
            pltpu.VMEM((2 * tiles, 128), F32),
            pltpu.VMEM((3 * tiles, 128), F32),
            pltpu.SMEM((1,), jnp.int32),
            pltpu.VMEM((8 * tiles, 128), F32),
            pltpu.VMEM((2, 12, CY, 128), F32),
            pltpu.VMEM((2, 12, CX, 128), F32),
            pltpu.VMEM((4, 16, 128), F32),
            pltpu.VMEM((LANE_TILES, 8, 128), F32),
            pltpu.VMEM((1, 128), F32),
            pltpu.VMEM((3, SW, 128), F32),
            dma((9,)), dma((24,)), dma((24,)),
        ],
        compiler_params=pltpu.CompilerParams(collective_id=0, has_side_effects=True, vmem_limit_bytes=20 << 20),
        name="exchange",
    )(*[pltpu.with_memory_space_constraint(v, pltpu.HBM) for v in (
        pops, anchor.reshape(tiles, 128), offsets.reshape(3 * tiles, 128),
        jnp.swapaxes(heading.reshape(2, tiles, 128), 0, 1).reshape(2 * tiles, 128),
        velocity.reshape(3 * tiles, 128))], live_count.reshape(1))
    moved, force = pl.pallas_call(
        fluid_kernel,
        out_shape=(jax.ShapeDtypeStruct((19, ROWS, NZ), F32), jax.ShapeDtypeStruct((3 * tiles, 128), F32)),
        in_specs=[vmem] * 12,
        out_specs=[hbm, hbm],
        scratch_shapes=[
            pltpu.VMEM((SW // OWN, 8, OWN), F32),
            pltpu.VMEM((19, ROWS, NZ), F32),
            pltpu.VMEM((3 * tiles, 128), F32),
            pltpu.SMEM((9, 1, 128), F32),
            pltpu.VMEM((7, ROWS, NZ), F32),
            pltpu.VMEM((3 * ADJ, 2 * NZ), BF16),
            pltpu.VMEM((3 * FAR_ROWS, 2 * NZ), BF16),
            pltpu.VMEM((3, ADJ_ROWS, NZ), F32),
            pltpu.VMEM((GHOST_TILES, 8, 128), F32),
            pltpu.VMEM((3, GHOST_TILES * 128, 128), F32),
            dma((19,)), dma, dma,
        ],
        compiler_params=pltpu.CompilerParams(vmem_limit_bytes=32 << 20),
        name="fluid",
    )(pops, own, base, halo_x, halo_y, halo_c, lists, starts, mom, inner, zhl, plane)
    return (moved.reshape(populations.shape), force.reshape(1, 1, 3, SW))


def solution(mesh):
    return jax.shard_map(
        functools.partial(body, mesh.shape["gx"], mesh.shape["gy"]),
        mesh=mesh,
        in_specs=(
            P(None, "gx", "gy", None),
            P("gx", "gy", None),
            P("gx", "gy", None, None),
            P("gx", "gy", None, None),
            P("gx", "gy", None, None),
            P("gx", "gy"),
        ),
        out_specs=(P(None, "gx", "gy", None), P("gx", "gy", None, None)),
        check_vma=False,
    )
```

profile of v0, /device:TPU:64, one launch (start us, length us, event | category | flops | bytes accessed | tf_op | source)
XLA Modules:
  0.0 30.0 jit_solution(5235494974380696798)
XLA Ops:
  1.3 24.0 %exchange.1 = (f32[19,128,128]{2,1,0:T(8,128)S(1)}, f32[2,12,16,128]{3,2,1,0:T(8,128)S(1)}, f32[2,12,8,128]{3,2,1,0:T(8,128)S(1)}, f32[4,16,128]{2,1,0:T(8,128)S...) custom-call(f32[19,128,128]{2,1,0:T(8,128)} %bitcast.13, ...), custom_call_target="tpu_custom_call" | custom-call | tf_op jit(solution)/shard_map/exchange/pallas_call | solution.py:580
  25.3 4.7 %fluid.1 = (f32[19,128,128]{2,1,0:T(8,128)}, f32[24,128]{1,0:T(8,128)}) custom-call(f32[19,128,128]{2,1,0:T(8,128)S(1)} %get-tuple-element.16.pops, f32[4,8,256]{2,1,0:T(8,128)S(1)} %get-tuple-element.17.own, f32[4,8,256]{2,1,0:T(8,128)S(1)} %get-tuple-element.18.base, f32[2,12,16,128]{3,2,1,0:T(8,128)S(1)} %get-tuple-element.19.halo_x, ...), custom_call_target="tpu_custom_call" | custom-call | tf_op jit(solution)/shard_map/fluid/pallas_call | solution.py:606
where the time goes:
time: 30.1 us; the launch traced here: 30 us
  Pallas kernels  28.7 us (95%)
  between operations  1.29 us (4%)
    pallas_call x1, Pallas kernels, body(): pl.pallas_call(functools.partial(exchange_kernel, n_gx, n_gy), out_shape=...  24 us
    pallas_call x1, Pallas kernels, body(): pl.pallas_call(fluid_kernel, out_shape=(jax.ShapeDtypeStruct((19, ROWS, N...  4.74 us

commit v1 on v0

--- a/solution.py
+++ b/solution.py
@@ -169,7 +169,7 @@
 def exchange_kernel(n_gx, n_gy, pops_hbm, anchor_hbm, offsets_hbm, heading_hbm, velocity_hbm, count_hbm,
                     pops, halo_x, halo_y, halo_c, lists, starts_out, own_out, base_out, mom, inner, zhl, plane,
                     anchor, offsets, heading, velocity, count, table,
-                    msg_x, msg_y, msg_c, msg_l, msg_s, cols, load_sem, send_sem, recv_sem):
+                    msg_x, msg_y, msg_c, msg_l, msg_s, cols, load_sem, send_sem, recv_sem, lower):
     gx = lax.axis_index("gx")
     gy = lax.axis_index("gy")
 
@@ -185,9 +185,52 @@
         c.start()
     barrier = pltpu.get_barrier_semaphore()
     for side in SIDES:
-        pl.semaphore_signal(barrier, inc=1, device_id=device(side), device_id_type=MESH)
+        if side[0] <= 0:
+            pl.semaphore_signal(barrier, inc=1, device_id=device(side), device_id_type=MESH)
     for c in loads:
         c.wait()
+
+    rho, m = moments(lambda q: pops[q])
+    inv = 1.0 / rho
+    mom[0] = rho
+    for c in range(3):
+        mom[1 + c] = m[c] * inv
+    for s, (adj, far) in enumerate(((0, 1), (CX - 1, CX - 2))):
+        for c in range(4):
+            msg_x[s, c] = mom[c, adj * CY:(adj + 1) * CY]
+        for c in range(3):
+            msg_x[s, 4 + c] = mom[1 + c, far * CY:(far + 1) * CY]
+        for k, q in enumerate(facing(0, 2 * s - 1)):
+            msg_x[s, 7 + k] = pops[q, adj * CY:(adj + 1) * CY]
+
+    def send(k, a, b, side, o):
+        d = SIDES.index(side)
+        return pltpu.make_async_remote_copy(
+            src_ref=a, dst_ref=b, send_sem=send_sem.at[3 * d + k], recv_sem=recv_sem.at[3 * o + k],
+            device_id=device(side), device_id_type=MESH)
+
+    copies = {}
+    for d, side in enumerate(SIDES):
+        o = SIDES.index((-side[0], -side[1]))
+        if side[1] == 0:
+            first = send(0, msg_x.at[d], halo_x.at[o], side, o)
+        elif side[0] == 0:
+            first = send(0, msg_y.at[d - 2], halo_y.at[o - 2], side, o)
+        else:
+            first = send(0, msg_c.at[d - 4], halo_c.at[o - 4], side, o)
+        copies[side] = (first, send(1, msg_s, starts_out.at[o], side, o),
+                        send(2, msg_l.at[:, pl.ds(0, 6)], lists.at[o, :, pl.ds(0, 6)], side, o))
+
+    def start(*sides):
+        for k in range(3):
+            for side in sides:
+                copies[side][k].start()
+
+    pl.semaphore_wait(barrier, 5)
+    for side in SIDES:
+        if side[0] > 0:
+            pl.semaphore_signal(lower, inc=1, device_id=device(side), device_id_type=MESH)
+    copies[(1, 0)][0].start()
 
     root = anchor[...]
     bxf = lax.shift_right_logical(root, 7).astype(F32)
@@ -226,18 +269,6 @@
         at = 24 * t
         msg_l[t] = ordered[at:at + 8] + ordered[at + 8:at + 16] + ordered[at + 16:at + 24]
 
-    rho, m = moments(lambda q: pops[q])
-    inv = 1.0 / rho
-    mom[0] = rho
-    for c in range(3):
-        mom[1 + c] = m[c] * inv
-    for s, (adj, far) in enumerate(((0, 1), (CX - 1, CX - 2))):
-        for c in range(4):
-            msg_x[s, c] = mom[c, adj * CY:(adj + 1) * CY]
-        for c in range(3):
-            msg_x[s, 4 + c] = mom[1 + c, far * CY:(far + 1) * CY]
-        for k, q in enumerate(facing(0, 2 * s - 1)):
-            msg_x[s, 7 + k] = pops[q, adj * CY:(adj + 1) * CY]
     for s, (adj, far) in enumerate(((0, 1), (CY - 1, CY - 2))):
         for c in range(4):
             msg_y[s, c] = mom[c, pl.ds(adj, CX, stride=CY)]
@@ -258,26 +289,12 @@
         q = DIRS.index((sx, sy, 0))
         msg_c[i, 4:5] = pops[q, ax * CY + ay:ax * CY + ay + 1]
 
-    def send(k, a, b, side, o):
-        d = SIDES.index(side)
-        return pltpu.make_async_remote_copy(
-            src_ref=a, dst_ref=b, send_sem=send_sem.at[3 * d + k], recv_sem=recv_sem.at[3 * o + k],
-            device_id=device(side), device_id_type=MESH)
-
-    fluid, swimmers = [], []
-    for d, side in enumerate(SIDES):
-        o = SIDES.index((-side[0], -side[1]))
-        if side[1] == 0:
-            fluid.append(send(0, msg_x.at[d], halo_x.at[o], side, o))
-        elif side[0] == 0:
-            fluid.append(send(0, msg_y.at[d - 2], halo_y.at[o - 2], side, o))
-        else:
-            fluid.append(send(0, msg_c.at[d - 4], halo_c.at[o - 4], side, o))
-        swimmers.append(send(1, msg_s, starts_out.at[o], side, o))
-        swimmers.append(send(2, msg_l.at[:, pl.ds(0, 6)], lists.at[o, :, pl.ds(0, 6)], side, o))
-    pl.semaphore_wait(barrier, 8)
-    for c in fluid + swimmers:
-        c.start()
+    copies[(1, 0)][1].start()
+    copies[(1, 0)][2].start()
+
+    @pl.when(gx == n_gx - 1)
+    def _():
+        start((1, -1), (1, 1))
 
     for c in range(3):
         inner[c * ROWS:(c + 1) * ROWS] = widen(mom[1 + c])
@@ -297,25 +314,44 @@
         for j in range(BLOCK // OWN):
             own_out[i * (BLOCK // OWN) + j] = rows[:, j * OWN:(j + 1) * OWN]
 
-    for t in range(LANE_TILES):
-        v = table[8 * t:8 * t + 8]
-        columns(cols, t * 128, jnp.where((sub == 0) & (v[6:7] == 0.0), FAR, v))
-    for i in range(0, SW // OWN, 2):
-        width = 2 * OWN
-        mine = [jnp.broadcast_to(jnp.concatenate([own_out[i, c:c + 1], own_out[i + 1, c:c + 1]], axis=1), (8, width))
-                for c in range(3)]
-        init = tuple(jnp.zeros((8, width), F32) for _ in range(3))
-        got = lax.fori_loop(0, SW // 8, pair_step(cols, mine, width), init)
-        for c in range(3):
-            pairs = 0.24 * jnp.sum(got[c], axis=0, keepdims=True)
-            for j in range(2):
-                base_out[i + j, c:c + 1] = (pairs[:, j * OWN:(j + 1) * OWN] * own_out[i + j, 6:7]
-                                            - own_out[i + j, 3 + c:4 + c])
-    for i in range(SW // OWN):
-        base_out[i, 3:8] = jnp.zeros((5, OWN), F32)
-
-    for c in fluid + swimmers:
-        c.wait()
+    def own_pairs():
+        for t in range(LANE_TILES):
+            v = table[8 * t:8 * t + 8]
+            columns(cols, t * 128, jnp.where((sub == 0) & (v[6:7] == 0.0), FAR, v))
+        for i in range(0, SW // OWN, 2):
+            width = 2 * OWN
+            mine = [jnp.broadcast_to(jnp.concatenate([own_out[i, c:c + 1], own_out[i + 1, c:c + 1]], axis=1), (8, width))
+                    for c in range(3)]
+            init = tuple(jnp.zeros((8, width), F32) for _ in range(3))
+            got = lax.fori_loop(0, SW // 8, pair_step(cols, mine, width), init)
+            for c in range(3):
+                pairs = 0.24 * jnp.sum(got[c], axis=0, keepdims=True)
+                for j in range(2):
+                    base_out[i + j, c:c + 1] = (pairs[:, j * OWN:(j + 1) * OWN] * own_out[i + j, 6:7]
+                                                - own_out[i + j, 3 + c:4 + c])
+        for i in range(SW // OWN):
+            base_out[i, 3:8] = jnp.zeros((5, OWN), F32)
+
+    start((0, -1), (0, 1))
+
+    @pl.when(gx != n_gx - 1)
+    def _():
+        start((1, -1), (1, 1))
+
+    @pl.when(gx == 0)
+    def _():
+        own_pairs()
+
+    pl.semaphore_wait(lower, 3)
+    start((-1, 0), (-1, -1), (-1, 1))
+
+    @pl.when(gx != 0)
+    def _():
+        own_pairs()
+
+    for side in SIDES:
+        for c in copies[side]:
+            c.wait()
 
 
 ADJ = 64
@@ -595,7 +631,7 @@
             pltpu.VMEM((LANE_TILES, 8, 128), F32),
             pltpu.VMEM((1, 128), F32),
             pltpu.VMEM((3, SW, 128), F32),
-            dma((9,)), dma((24,)), dma((24,)),
+            dma((9,)), dma((24,)), dma((24,)), pltpu.SemaphoreType.REGULAR,
         ],
         compiler_params=pltpu.CompilerParams(collective_id=0, has_side_effects=True, vmem_limit_bytes=20 << 20),
         name="exchange",

time: 30.1 us -> 28.9 us (0.960)
  Pallas kernels: 28.7 us -> 27.6 us
    pallas_call x1, Pallas kernels: 24 us -> 22.8 us  [body(): pl.pallas_call(functools.partial(exchange_kernel, n_gx, n_gy), out_shape=...]
where the time goes in v1:
time: 28.9 us
  Pallas kernels  27.6 us (96%)
  between operations  1.29 us (4%)
    pallas_call x1, Pallas kernels, body(): pl.pallas_call(functools.partial(exchange_kernel, n_gx, n_gy), out_shape=...  22.8 us
    pallas_call x1, Pallas kernels, body(): pl.pallas_call(fluid_kernel, out_shape=(jax.ShapeDtypeStruct((19, ROWS, N...  4.81 us

profile of v1, /device:TPU:64, one launch (start us, length us, event | category | flops | bytes accessed | tf_op | source)
XLA Modules:
  0.0 28.9 jit_solution(16311554129661155922)
XLA Ops:
  1.3 22.8 %exchange.1 = (f32[19,128,128]{2,1,0:T(8,128)S(1)}, f32[2,12,16,128]{3,2,1,0:T(8,128)S(1)}, f32[2,12,8,128]{3,2,1,0:T(8,128)S(1)}, f32[4,16,128]{2,1,0:T(8,128)S...) custom-call(f32[19,128,128]{2,1,0:T(8,128)} %bitcast.13, ...), custom_call_target="tpu_custom_call" | custom-call | tf_op jit(solution)/shard_map/exchange/pallas_call | solution.py:616
  24.1 4.8 %fluid.1 = (f32[19,128,128]{2,1,0:T(8,128)}, f32[24,128]{1,0:T(8,128)}) custom-call(f32[19,128,128]{2,1,0:T(8,128)S(1)} %get-tuple-element.16.pops, f32[4,8,256]{2,1,0:T(8,128)S(1)} %get-tuple-element.17.own, f32[4,8,256]{2,1,0:T(8,128)S(1)} %get-tuple-element.18.base, f32[2,12,16,128]{3,2,1,0:T(8,128)S(1)} %get-tuple-element.19.halo_x, ...), custom_call_target="tpu_custom_call" | custom-call | tf_op jit(solution)/shard_map/fluid/pallas_call | solution.py:642

commit v2 on v0

--- a/solution.py
+++ b/solution.py
@@ -169,7 +169,7 @@
 def exchange_kernel(n_gx, n_gy, pops_hbm, anchor_hbm, offsets_hbm, heading_hbm, velocity_hbm, count_hbm,
                     pops, halo_x, halo_y, halo_c, lists, starts_out, own_out, base_out, mom, inner, zhl, plane,
                     anchor, offsets, heading, velocity, count, table,
-                    msg_x, msg_y, msg_c, msg_l, msg_s, cols, load_sem, send_sem, recv_sem):
+                    msg_x, msg_y, msg_c, msg_l, msg_s, cols, load_sem, send_sem, recv_sem, lower):
     gx = lax.axis_index("gx")
     gy = lax.axis_index("gy")
 
@@ -185,8 +185,9 @@
         c.start()
     barrier = pltpu.get_barrier_semaphore()
     for side in SIDES:
-        pl.semaphore_signal(barrier, inc=1, device_id=device(side), device_id_type=MESH)
-    for c in loads:
+        if side[0] <= 0:
+            pl.semaphore_signal(barrier, inc=1, device_id=device(side), device_id_type=MESH)
+    for c in loads[:5]:
         c.wait()
 
     root = anchor[...]
@@ -226,6 +227,45 @@
         at = 24 * t
         msg_l[t] = ordered[at:at + 8] + ordered[at + 8:at + 16] + ordered[at + 16:at + 24]
 
+    def send(k, a, b, side, o):
+        d = SIDES.index(side)
+        return pltpu.make_async_remote_copy(
+            src_ref=a, dst_ref=b, send_sem=send_sem.at[3 * d + k], recv_sem=recv_sem.at[3 * o + k],
+            device_id=device(side), device_id_type=MESH)
+
+    copies = {}
+    for d, side in enumerate(SIDES):
+        o = SIDES.index((-side[0], -side[1]))
+        if side[1] == 0:
+            first = send(0, msg_x.at[d], halo_x.at[o], side, o)
+        elif side[0] == 0:
+            first = send(0, msg_y.at[d - 2], halo_y.at[o - 2], side, o)
+        else:
+            first = send(0, msg_c.at[d - 4], halo_c.at[o - 4], side, o)
+        copies[side] = (first, send(1, msg_s, starts_out.at[o], side, o),
+                        send(2, msg_l.at[:, pl.ds(0, 6)], lists.at[o, :, pl.ds(0, 6)], side, o))
+
+    def start(sides, kinds=(0, 1, 2)):
+        for k in kinds:
+            for side in sides:
+                copies[side][k].start()
+
+    corners_up, along_y, down = ((1, -1), (1, 1)), ((0, -1), (0, 1)), ((-1, 0), (-1, -1), (-1, 1))
+    last = gx == n_gx - 1
+    late = gx >= n_gx - max(n_gx // 4, 1)
+    pl.semaphore_wait(barrier, 5)
+    for side in SIDES:
+        if side[0] > 0:
+            pl.semaphore_signal(lower, inc=1, device_id=device(side), device_id_type=MESH)
+
+    @pl.when(last)
+    def _():
+        start(corners_up, (1, 2))
+
+    start(((1, 0),), (1, 2))
+
+    for c in loads[5:]:
+        c.wait()
     rho, m = moments(lambda q: pops[q])
     inv = 1.0 / rho
     mom[0] = rho
@@ -238,13 +278,7 @@
             msg_x[s, 4 + c] = mom[1 + c, far * CY:(far + 1) * CY]
         for k, q in enumerate(facing(0, 2 * s - 1)):
             msg_x[s, 7 + k] = pops[q, adj * CY:(adj + 1) * CY]
-    for s, (adj, far) in enumerate(((0, 1), (CY - 1, CY - 2))):
-        for c in range(4):
-            msg_y[s, c] = mom[c, pl.ds(adj, CX, stride=CY)]
-        for c in range(3):
-            msg_y[s, 4 + c] = mom[1 + c, pl.ds(far, CX, stride=CY)]
-        for k, q in enumerate(facing(1, 2 * s - 1)):
-            msg_y[s, 7 + k] = pops[q, pl.ds(adj, CX, stride=CY)]
+
     for i in range(4):
         sx, sy = SIDES[4 + i]
         ax, fx = (0, 1) if sx < 0 else (CX - 1, CX - 2)
@@ -258,26 +292,48 @@
         q = DIRS.index((sx, sy, 0))
         msg_c[i, 4:5] = pops[q, ax * CY + ay:ax * CY + ay + 1]
 
-    def send(k, a, b, side, o):
-        d = SIDES.index(side)
-        return pltpu.make_async_remote_copy(
-            src_ref=a, dst_ref=b, send_sem=send_sem.at[3 * d + k], recv_sem=recv_sem.at[3 * o + k],
-            device_id=device(side), device_id_type=MESH)
-
-    fluid, swimmers = [], []
-    for d, side in enumerate(SIDES):
-        o = SIDES.index((-side[0], -side[1]))
-        if side[1] == 0:
-            fluid.append(send(0, msg_x.at[d], halo_x.at[o], side, o))
-        elif side[0] == 0:
-            fluid.append(send(0, msg_y.at[d - 2], halo_y.at[o - 2], side, o))
-        else:
-            fluid.append(send(0, msg_c.at[d - 4], halo_c.at[o - 4], side, o))
-        swimmers.append(send(1, msg_s, starts_out.at[o], side, o))
-        swimmers.append(send(2, msg_l.at[:, pl.ds(0, 6)], lists.at[o, :, pl.ds(0, 6)], side, o))
-    pl.semaphore_wait(barrier, 8)
-    for c in fluid + swimmers:
-        c.start()
+
+    @pl.when(last)
+    def _():
+        start(corners_up, (0,))
+
+    start(((1, 0),), (0,))
+    for s, (adj, far) in enumerate(((0, 1), (CY - 1, CY - 2))):
+        for c in range(4):
+            msg_y[s, c] = mom[c, pl.ds(adj, CX, stride=CY)]
+        for c in range(3):
+            msg_y[s, 4 + c] = mom[1 + c, pl.ds(far, CX, stride=CY)]
+        for k, q in enumerate(facing(1, 2 * s - 1)):
+            msg_y[s, 7 + k] = pops[q, pl.ds(adj, CX, stride=CY)]
+    def own_pairs():
+        for t in range(LANE_TILES):
+            v = table[8 * t:8 * t + 8]
+            columns(cols, t * 128, jnp.where((sub == 0) & (v[6:7] == 0.0), FAR, v))
+        for i in range(0, SW // OWN, 2):
+            width = 2 * OWN
+            mine = [jnp.broadcast_to(jnp.concatenate([own_out[i, c:c + 1], own_out[i + 1, c:c + 1]], axis=1), (8, width))
+                    for c in range(3)]
+            init = tuple(jnp.zeros((8, width), F32) for _ in range(3))
+            got = lax.fori_loop(0, SW // 8, pair_step(cols, mine, width), init)
+            for c in range(3):
+                pairs = 0.24 * jnp.sum(got[c], axis=0, keepdims=True)
+                for j in range(2):
+                    base_out[i + j, c:c + 1] = (pairs[:, j * OWN:(j + 1) * OWN] * own_out[i + j, 6:7]
+                                                - own_out[i + j, 3 + c:4 + c])
+        for i in range(SW // OWN):
+            base_out[i, 3:8] = jnp.zeros((5, OWN), F32)
+
+    def send_down():
+        pl.semaphore_wait(lower, 3)
+        start(down)
+
+    @pl.when(jnp.logical_not(late))
+    def _():
+        start(along_y + corners_up)
+
+    @pl.when(jnp.logical_not(late) & (gx != 0))
+    def _():
+        send_down()
 
     for c in range(3):
         inner[c * ROWS:(c + 1) * ROWS] = widen(mom[1 + c])
@@ -297,25 +353,27 @@
         for j in range(BLOCK // OWN):
             own_out[i * (BLOCK // OWN) + j] = rows[:, j * OWN:(j + 1) * OWN]
 
-    for t in range(LANE_TILES):
-        v = table[8 * t:8 * t + 8]
-        columns(cols, t * 128, jnp.where((sub == 0) & (v[6:7] == 0.0), FAR, v))
-    for i in range(0, SW // OWN, 2):
-        width = 2 * OWN
-        mine = [jnp.broadcast_to(jnp.concatenate([own_out[i, c:c + 1], own_out[i + 1, c:c + 1]], axis=1), (8, width))
-                for c in range(3)]
-        init = tuple(jnp.zeros((8, width), F32) for _ in range(3))
-        got = lax.fori_loop(0, SW // 8, pair_step(cols, mine, width), init)
-        for c in range(3):
-            pairs = 0.24 * jnp.sum(got[c], axis=0, keepdims=True)
-            for j in range(2):
-                base_out[i + j, c:c + 1] = (pairs[:, j * OWN:(j + 1) * OWN] * own_out[i + j, 6:7]
-                                            - own_out[i + j, 3 + c:4 + c])
-    for i in range(SW // OWN):
-        base_out[i, 3:8] = jnp.zeros((5, OWN), F32)
-
-    for c in fluid + swimmers:
-        c.wait()
+    @pl.when(late)
+    def _():
+        start(along_y)
+
+    @pl.when(late & jnp.logical_not(last))
+    def _():
+        start(corners_up)
+
+    @pl.when(late)
+    def _():
+        send_down()
+
+    own_pairs()
+
+    @pl.when(gx == 0)
+    def _():
+        send_down()
+
+    for side in SIDES:
+        for c in copies[side]:
+            c.wait()
 
 
 ADJ = 64
@@ -595,7 +653,7 @@
             pltpu.VMEM((LANE_TILES, 8, 128), F32),
             pltpu.VMEM((1, 128), F32),
             pltpu.VMEM((3, SW, 128), F32),
-            dma((9,)), dma((24,)), dma((24,)),
+            dma((9,)), dma((24,)), dma((24,)), pltpu.SemaphoreType.REGULAR,
         ],
         compiler_params=pltpu.CompilerParams(collective_id=0, has_side_effects=True, vmem_limit_bytes=20 << 20),
         name="exchange",

time: 30.1 us -> 29.1 us (0.967)
  the two profiles are of different devices: /device:TPU:64 before, /device:TPU:40 now
where the time goes in v2:
time: 29.1 us; the launch traced here: 28.9 us
  Pallas kernels  27.6 us (95%)
  between operations  1.29 us (4%)
    pallas_call x1, Pallas kernels, body(): pl.pallas_call(functools.partial(exchange_kernel, n_gx, n_gy), out_shape=...  23 us
    pallas_call x1, Pallas kernels, body(): pl.pallas_call(fluid_kernel, out_shape=(jax.ShapeDtypeStruct((19, ROWS, N...  4.53 us

profile of v2, /device:TPU:40, one launch (start us, length us, event | category | flops | bytes accessed | tf_op | source)
XLA Modules:
  0.0 28.9 jit_solution(17409524016204307879)
XLA Ops:
  1.3 23.0 %exchange.1 = (f32[19,128,128]{2,1,0:T(8,128)S(1)}, f32[2,12,16,128]{3,2,1,0:T(8,128)S(1)}, f32[2,12,8,128]{3,2,1,0:T(8,128)S(1)}, f32[4,16,128]{2,1,0:T(8,128)S...) custom-call(f32[19,128,128]{2,1,0:T(8,128)} %bitcast.13, ...), custom_call_target="tpu_custom_call" | custom-call | tf_op jit(solution)/shard_map/exchange/pallas_call | solution.py:638
  24.3 4.5 %fluid.1 = (f32[19,128,128]{2,1,0:T(8,128)}, f32[24,128]{1,0:T(8,128)}) custom-call(f32[19,128,128]{2,1,0:T(8,128)S(1)} %get-tuple-element.16.pops, f32[4,8,256]{2,1,0:T(8,128)S(1)} %get-tuple-element.17.own, f32[4,8,256]{2,1,0:T(8,128)S(1)} %get-tuple-element.18.base, f32[2,12,16,128]{3,2,1,0:T(8,128)S(1)} %get-tuple-element.19.halo_x, ...), custom_call_target="tpu_custom_call" | custom-call | tf_op jit(solution)/shard_map/fluid/pallas_call | solution.py:664
